TPU v7x, 256 devices: a whole 4x4x8 slice. The times are simulated.
256 devices in a mesh: wide: 64 (over y, z_lo, x), layer: 4 (over z_hi, core).
Axes of the slice: x: 4, y: 4, z: 8 (z_hi: 2, z_lo: 4; z = z_hi * 4 + z_lo), core: 2. Of those that a mesh axis runs over, the one named last changes fastest.
Arguments:
- factor: float32 [32768, 8192], P('layer', 'wide'), parts along dimension 0, may hold values from -1 to 21, as said below
Outputs:
- rotated: float32 [32768, 8192], P('layer', 'wide'), parts along dimension 0
- eigen_basis: float32 [32768, 8192], P('layer', 'wide'), parts along dimension 0
There are 4 independent parts, one for each index of `layer`. A program takes and returns all parts, laid end to end along the dimension named above; each array names one. Nothing has to cross between parts.
Inputs may be any that keep to these rules, and one draw needn't show every extreme that they name: `factor`: symmetric.
All inputs are finite; a program needn't handle non-finite values.
Results may differ from a plain program's by a relative error of at most 0.00095.
Values sent between devices are 32-bit elements; how exact they have to be, the bound alone decides.
A program may use at most 128 MiB of HBM per device.

v0:
```python
import jax
import jax.numpy as jnp
from jax import lax
from jax.sharding import Mesh
from jax.sharding import PartitionSpec as P

SWEEPS = 3
WIDE = ("wide_0", "wide_1", "wide_2")
floor_term = 0.01


def laid_out(parts, dim):
    dims = list(parts.shape[1:])
    dims[dim] *= parts.shape[0]
    return jnp.moveaxis(parts, 0, dim).reshape(dims)


def gather_in_order(shard, axes, order):
    parts = shard[None]
    for k in order:
        parts = lax.all_gather(parts, axes[k], axis=0, tiled=True)
    held = [lax.axis_size(axes[k]) for k in reversed(order)]
    parts = parts.reshape(*held, *shard.shape)
    turned = sorted(range(len(order)), key=lambda place: order[len(order) - 1 - place])
    return parts.transpose(*turned, *range(len(order), parts.ndim)).reshape(-1, *shard.shape)


def whole_of(shard, axes, order, dim):
    return laid_out(gather_in_order(shard, axes, order), dim)


def from_partner(shard, axis, bit):
    return lax.ppermute(shard, axis, [(i, i ^ 1 << bit) for i in range(lax.axis_size(axis))])


def cayley_sweeps(pair_block):
    order_size = pair_block.shape[0]
    identity_mat = jnp.eye(order_size, dtype=pair_block.dtype)
    rotation = identity_mat
    for repeat in range(SWEEPS):
        diagonal = jnp.diagonal(pair_block)
        spread = diagonal[None, :] - diagonal[:, None]
        ratios = (
            pair_block * spread / (spread * spread + 2.0 * pair_block * pair_block + floor_term)
        )
        skewed = 0.5 * (ratios - ratios.T) * (1.0 - identity_mat)
        half_turn = identity_mat + 0.5 * skewed
        system = identity_mat - 0.25 * jnp.dot(skewed, skewed, precision=lax.Precision.HIGHEST)
        lower_part = jnp.linalg.cholesky(system)
        square_turn = jnp.dot(half_turn, half_turn, precision=lax.Precision.HIGHEST)
        rotate_now = jax.scipy.linalg.cho_solve((lower_part, True), square_turn)
        pair_block = jnp.dot(
            rotate_now.T,
            jnp.dot(pair_block, rotate_now, precision=lax.Precision.HIGHEST),
            precision=lax.Precision.HIGHEST,
        )
        rotation = jnp.dot(rotation, rotate_now, precision=lax.Precision.HIGHEST)
    return rotation


def trade_rows(current, wide_count, width_half):
    order_size, pair_span = current.shape
    split_view = current.reshape(2, wide_count // 2, 2, width_half, pair_span)
    joined = jnp.concatenate([split_view[:, :, :1], split_view[::-1, :, 1:]], axis=2)
    return joined.reshape(order_size, pair_span)


def one_round(current, basis, my_pair):
    order_size, pair_span = current.shape
    pair_block = lax.dynamic_slice_in_dim(current, my_pair * pair_span, pair_span, 0)
    rotate = cayley_sweeps(pair_block)
    columns = jnp.dot(current, rotate, precision=lax.Precision.HIGHEST)
    pieces = whole_of(rotate[None], WIDE, (1, 0, 2), 0)
    how_many = pieces.shape[0]
    row_slab = columns
    row_slab = row_slab.reshape(how_many, pair_span, pair_span)
    updated = jnp.einsum("nba,nbc->nac", pieces, row_slab, precision=lax.Precision.HIGHEST)
    current = lax.dynamic_update_slice_in_dim(
        columns, updated.reshape(how_many * pair_span, pair_span), jnp.int32(0) * pair_span, 0
    )
    basis = jnp.dot(basis, rotate, precision=lax.Precision.HIGHEST)
    return (current, basis)


def body(factor):
    wide_count = lax.axis_size(WIDE)
    my_pair = lax.axis_index(WIDE)
    order_size, pair_span = factor.shape
    width_half = pair_span // 2
    row_index = lax.broadcasted_iota(jnp.int32, (order_size, pair_span), 0)
    col_index = lax.broadcasted_iota(jnp.int32, (order_size, pair_span), 1) + my_pair * pair_span
    basis = (row_index == col_index).astype(jnp.float32)
    current = factor
    for repeat in range(2):
        if repeat == 1:
            moved_factor, moved_basis = from_partner(
                (current[:, width_half:], basis[:, width_half:]), WIDE, wide_count.bit_length() - 2
            )
            current = jnp.concatenate([current[:, :width_half], moved_factor], axis=1)
            basis = jnp.concatenate([basis[:, :width_half], moved_basis], axis=1)
            current = trade_rows(current, wide_count, width_half)
        current, basis = one_round(current, basis, my_pair)
    return (current, basis)


def solution(mesh):
    finer = Mesh(
        mesh.devices.reshape(4, 4, 4, mesh.shape["layer"]), ("wide_0", "wide_1", "wide_2", "layer")
    )
    in_specs = (P("layer", WIDE),)
    out_specs = (P("layer", WIDE), P("layer", WIDE))
    return jax.shard_map(body, mesh=finer, in_specs=in_specs, out_specs=out_specs, check_vma=False)
```

profile of v0, /device:TPU:2, one launch (start us, length us, event | category | flops | bytes accessed | tf_op | source)
XLA Modules:
  0.0 474.6 jit_solution(8822284381728006457)
XLA Ops:
  10.3 11.7 %cholesky.104 = f32[128,128]{1,0:T(8,128)S(1)} custom-call(f32[128,128]{1,0:T(8,128)S(1)} %fusion.100), custom_call_target="Cholesky" | custom-call | tf_op jit(solution)/shard_map/jit(cholesky)/cholesky | solution.py:49
  23.4 9.8 %custom-call.24 = f32[1,128,128]{1,2,0:T(8,128)S(1)} custom-call(f32[1,128,128]{2,1,0:T(8,128)S(1)} %fusion.18), custom_call_target="InvertDiagBlocksLowerTriangular" | custom-call | tf_op jit(solution)/shard_map/jit(_cho_solve)/triangular_solve | solution.py:51
  37.0 11.7 %cholesky.115 = f32[128,128]{1,0:T(8,128)S(1)} custom-call(f32[128,128]{1,0:T(8,128)S(1)} %fusion.95), custom_call_target="Cholesky" | custom-call | tf_op jit(solution)/shard_map/jit(cholesky)/cholesky | solution.py:49
  50.1 9.8 %custom-call.25 = f32[1,128,128]{1,2,0:T(8,128)S(1)} custom-call(f32[1,128,128]{2,1,0:T(8,128)S(1)} %fusion.19), custom_call_target="InvertDiagBlocksLowerTriangular" | custom-call | tf_op jit(solution)/shard_map/jit(_cho_solve)/triangular_solve | solution.py:51
  63.4 11.7 %cholesky.126 = f32[128,128]{1,0:T(8,128)S(1)} custom-call(f32[128,128]{1,0:T(8,128)S(1)} %fusion.90), custom_call_target="Cholesky" | custom-call | tf_op jit(solution)/shard_map/jit(cholesky)/cholesky | solution.py:49
  76.4 9.8 %custom-call.26 = f32[1,128,128]{1,2,0:T(8,128)S(1)} custom-call(f32[1,128,128]{2,1,0:T(8,128)S(1)} %fusion.20), custom_call_target="InvertDiagBlocksLowerTriangular" | custom-call | tf_op jit(solution)/shard_map/jit(_cho_solve)/triangular_solve | solution.py:51
  86.9 15.6 %all-gather = f32[512,128]{1,0:T(8,128)} all-gather(f32[128,128]{1,0:T(8,128)S(1)} %fusion.147), channel_id=2, replica_groups=mesh['wide_0'=4,'wide_1'=4,'wide_2'=4,'layer'=4] {'wide_1'}, dimensions={0}, use_global_device_ids=true | all-gather | bytes 327680 | tf_op jit(solution)/shard_map/all_gather | solution.py:21
  102.6 28.8 %all-gather.7.cloned.1.call-done = f32[16,1,128,128]{3,2,1,0:T(8,128)} async-done(((f32[4,1,128,128]{3,2,1,0:T(8,128)}), f32[16,1,128,128]{3,2,1,0:T(8,128)}) %all-gather.7.cloned.1.call-update) | async-done | bytes 1048592 | tf_op jit(solution)/shard_map/all_gather | solution.py:21
  131.4 8.1 %convolution_bitcast_fusion = f32[8192,128]{0,1:T(8,128)} fusion(f32[128,128]{1,0:T(8,128)S(1)} %fusion.147, f32[8192,128]{1,0:T(8,128)} %param.4), kind=kOutput, calls=%fused_computation.6 | convolution fusion | flops 1610612736 | bytes 8454144 | tf_op jit(solution)/shard_map/dot_general | solution.py:72
  139.5 5.8 %copy.106 = f32[8192,128]{1,0:T(8,128)} copy(f32[8192,128]{0,1:T(8,128)} %convolution_bitcast_fusion) | data formatting | bytes 8388608 | tf_op jit(solution)/shard_map/reshape | solution.py:76
  145.3 38.4 %all-gather.9.cloned.1.call-done = f32[64,1,128,128]{3,2,1,0:T(8,128)} async-done(((f32[16,1,128,128]{3,2,1,0:T(8,128)}), f32[64,1,128,128]{3,2,1,0:T(8,128)}) %all-gather.9.cloned.1.call-update) | async-done | bytes 4194320 | tf_op jit(solution)/shard_map/all_gather | solution.py:21
  183.7 5.2 %copy.80 = f32[4,4,4,1,128,128]{4,5,0,2,1,3:T(8,128)} copy(f32[4,4,4,1,128,128]{5,4,2,1,0,3:T(8,128)} %bitcast.185) | data formatting | bytes 8388608 | tf_op jit(solution)/shard_map/reshape | solution.py:23
  188.9 6.6 %fusion.148 = f32[64,128,128]{2,1,0:T(8,128)S(1)} fusion(f32[64,128,128]{1,2,0:T(8,128)} %bitcast.181, f32[64,128,128]{2,1,0:T(8,128)} %bitcast.179), kind=kOutput, calls=%fused_computation.227 | convolution fusion | flops 1610612736 | bytes 12582912 | tf_op jit(solution)/shard_map/nba,nbc->nac/dot_general | solution.py:77
  195.5 4.7 fusion.141
  200.2 2.8 copy.82
  203.1 3.1 collective-permute-start
  206.2 45.8 %collective-permute-done = f32[8192,64]{0,1:T(8,128)} collective-permute-done((f32[8192,64]{0,1:T(8,128)S(1)}, f32[8192,64]{0,1:T(8,128)}, u32[]{:S(2)}, u32[]{:S(2)}) %collective-permute-start) | collective-permute-done | bytes 2097184 | tf_op jit(solution)/shard_map/ppermute | solution.py:33
  252.0 3.8 copy.83
  255.8 4.6 pad_maximum_fusion
  270.4 11.7 %cholesky.137 = f32[128,128]{1,0:T(8,128)S(1)} custom-call(f32[128,128]{1,0:T(8,128)S(1)} %fusion.84), custom_call_target="Cholesky" | custom-call | tf_op jit(solution)/shard_map/jit(cholesky)/cholesky | solution.py:49
  283.4 9.8 %custom-call.27 = f32[1,128,128]{1,2,0:T(8,128)S(1)} custom-call(f32[1,128,128]{2,1,0:T(8,128)S(1)} %fusion.21), custom_call_target="InvertDiagBlocksLowerTriangular" | custom-call | tf_op jit(solution)/shard_map/jit(_cho_solve)/triangular_solve | solution.py:51
  297.0 11.7 %cholesky.148 = f32[128,128]{1,0:T(8,128)S(1)} custom-call(f32[128,128]{1,0:T(8,128)S(1)} %fusion.79), custom_call_target="Cholesky" | custom-call | tf_op jit(solution)/shard_map/jit(cholesky)/cholesky | solution.py:49
  310.1 9.8 %custom-call.28 = f32[1,128,128]{1,2,0:T(8,128)S(1)} custom-call(f32[1,128,128]{2,1,0:T(8,128)S(1)} %fusion.22), custom_call_target="InvertDiagBlocksLowerTriangular" | custom-call | tf_op jit(solution)/shard_map/jit(_cho_solve)/triangular_solve | solution.py:51
  323.4 11.7 %cholesky.159 = f32[128,128]{1,0:T(8,128)S(1)} custom-call(f32[128,128]{1,0:T(8,128)S(1)} %fusion.74), custom_call_target="Cholesky" | custom-call | tf_op jit(solution)/shard_map/jit(cholesky)/cholesky | solution.py:49
  336.4 9.8 %custom-call.29 = f32[1,128,128]{1,2,0:T(8,128)S(1)} custom-call(f32[1,128,128]{2,1,0:T(8,128)S(1)} %fusion.23), custom_call_target="InvertDiagBlocksLowerTriangular" | custom-call | tf_op jit(solution)/shard_map/jit(_cho_solve)/triangular_solve | solution.py:51
  346.9 14.8 %all-gather.1 = f32[512,128]{1,0:T(8,128)} all-gather(f32[128,128]{1,0:T(8,128)S(1)} %fusion.154), channel_id=3, replica_groups=mesh['wide_0'=4,'wide_1'=4,'wide_2'=4,'layer'=4] {'wide_1'}, dimensions={0}, use_global_device_ids=true | all-gather | bytes 327680 | tf_op jit(solution)/shard_map/all_gather | solution.py:21
  361.8 28.0 %all-gather.11.cloned.1.call-done = f32[16,1,128,128]{3,2,1,0:T(8,128)} async-done(((f32[4,1,128,128]{3,2,1,0:T(8,128)}), f32[16,1,128,128]{3,2,1,0:T(8,128)}) %all-gather.11.cloned.1.call-update) | async-done | bytes 1048592 | tf_op jit(solution)/shard_map/all_gather | solution.py:21
  394.6 44.7 %collective-permute-done.1 = f32[8192,64]{0,1:T(8,128)S(1)} collective-permute-done((f32[8192,64]{0,1:T(8,128)S(1)}, f32[8192,64]{0,1:T(8,128)S(1)}, u32[]{:S(2)}, u32[]{:S(2)}) %collective-permute-start.1) | collective-permute-done | bytes 2097184 | tf_op jit(solution)/shard_map/ppermute | solution.py:33
  439.3 8.5 %fusion = f32[8192,128]{1,0:T(8,128)} fusion(f32[128,128]{1,0:T(8,128)S(1)} %fusion.154, f32[8192,64]{0,1:T(8,128)S(1)} %collective-permute-done.1, f32[8192,64]{0,1:T(8,128)S(1)} %get-tuple-element.4), kind=kOutput, calls=%fused_computation.9 | convolution fusion | flops 1611661312 | bytes 8454144 | tf_op jit(solution)/shard_map/dot_general | solution.py:81
  447.8 4.9 %fusion.68 = f32[64,128,128]{2,1,0:T(8,128)} fusion(f32[64,128,128]{2,1,0:T(8,128)S(1)} %bitcast.178, f32[128,128]{1,0:T(8,128)S(1)} %fusion.154), kind=kOutput, calls=%fused_computation.127 | convolution fusion | flops 1610612736 | bytes 8454144 | tf_op jit(solution)/shard_map/dot_general | solution.py:72
  452.7 5.2 %copy.99 = f32[4,4,4,1,128,128]{4,5,0,2,1,3:T(8,128)} copy(f32[4,4,4,1,128,128]{5,4,2,1,0,3:T(8,128)} %bitcast.184) | data formatting | bytes 8388608 | tf_op jit(solution)/shard_map/reshape | solution.py:23
  458.0 9.9 %fusion.155 = f32[64,128,128]{2,1,0:T(8,128)} fusion(f32[64,128,128]{1,2,0:T(8,128)} %bitcast.182, f32[64,128,128]{2,1,0:T(8,128)} %fusion.68), kind=kOutput, calls=%fused_computation.234 | convolution fusion | flops 1610612736 | bytes 12582912 | tf_op jit(solution)/shard_map/nba,nbc->nac/dot_general | solution.py:77
  (111 shorter events, 41.4 us)
Async XLA Ops:
  7.2 124.2 %all-gather.7.cloned.1.call-start = ((), (), s32[]{:S(2)}) async-start(), calls=%async_computation | async-start | bytes 1310720 | tf_op jit(solution)/shard_map/all_gather | solution.py:21
  102.5 81.1 %all-gather.9.cloned.1.call-start = ((), (), s32[]{:S(2)}) async-start(), calls=%async_computation.1 | async-start | bytes 5242880 | tf_op jit(solution)/shard_map/all_gather | solution.py:21
  131.4 258.5 %all-gather.11.cloned.1.call-start = ((), (), s32[]{:S(2)}) async-start(), calls=%async_computation.2 | async-start | bytes 1310720 | tf_op jit(solution)/shard_map/all_gather | solution.py:21
  203.1 48.9 %collective-permute-start = (f32[8192,64]{0,1:T(8,128)S(1)}, f32[8192,64]{0,1:T(8,128)}, u32[]{:S(2)}, u32[]{:S(2)}) collective-permute-start(f32[8192,64]{0,1:T(8,128)S(1)} %copy.82), channel_id=1, source_target_pairs={{0,128},{4,132},{8,136},{12,140},{16,144},{20,148},{24,152},{28,15... | collective-permute-start | bytes 6291464 | tf_op jit(solution)/shard_map/ppermute | solution.py:33
  266.1 2.0 copy-start
  361.8 90.9 %all-gather.13.cloned.1.call-start = ((), (), s32[]{:S(2)}) async-start(), calls=%async_computation.3 | async-start | bytes 5242880 | tf_op jit(solution)/shard_map/all_gather | solution.py:21
  392.4 46.9 %collective-permute-start.1 = (f32[8192,64]{0,1:T(8,128)S(1)}, f32[8192,64]{0,1:T(8,128)S(1)}, u32[]{:S(2)}, u32[]{:S(2)}) collective-permute-start(f32[8192,64]{0,1:T(8,128)S(1)} %get-tuple-element.5), channel_id=1, source_target_pairs={{0,128},{4,132},{8,136},{12,140},{16,144},{20,148},{24,152},{28,15... | collective-permute-start | bytes 6291464 | tf_op jit(solution)/shard_map/ppermute | solution.py:33
  439.3 8.5 %copy-start.1 = (f32[2,32,2,64,128]{4,3,2,1,0:T(8,128)S(1)}, f32[2,32,2,64,128]{4,3,2,1,0:T(8,128)}, u32[]{:S(2)}) copy-start(f32[2,32,2,64,128]{4,3,2,1,0:T(8,128)} %copy-done) | copy-start | bytes 12582916
Sparse Core Ops, SparseCore 0:
  102.6 28.6 all-gather.6
  133.2 50.4 all-gather.8
  361.9 27.9 all-gather.10
  391.5 50.4 all-gather.12
where the time goes:
time: 481 us; the launch traced here: 475 us
  waiting for transfers between devices  186 us (39%)
  other arithmetic  145 us (30%)
  matrix products  49.3 us (10%)
  local copies, waits for them, and re-layouts  44 us (9%)
  blocking collectives  30.4 us (6%)
  between operations  14.7 us (3%)
  starting transfers between devices  5.42 us (1%)
    all_gather x4, waiting for transfers between devices, gather_in_order(): parts = lax.all_gather(parts, axes[k], axis=0, tiled=True)  95.2 us
    ppermute x2, waiting for transfers between devices, from_partner(): lax.ppermute(shard, axis, [(i, i ^ 1 << bit) for i in range(lax.axis_size...  90.5 us
    another operation x18, other arithmetic, cayley_sweeps(): lower_part = jnp.linalg.cholesky(system)  74.3 us
    another operation x12, other arithmetic, cayley_sweeps(): rotate_now = jax.scipy.linalg.cho_solve((lower_part, True), square_turn)  62.8 us
    all_gather x2, blocking collectives, gather_in_order(): parts = lax.all_gather(parts, axes[k], axis=0, tiled=True)  30.4 us
    dot_general x2, matrix products, one_round(): jnp.einsum('nba,nbc->nac', pieces, row_slab, precision=lax.Precision.HIGH...  16.5 us
    dot_general x2, matrix products, one_round(): columns = jnp.dot(current, rotate, precision=lax.Precision.HIGHEST)  13 us
    dot_general x2, matrix products, one_round(): basis = jnp.dot(basis, rotate, precision=lax.Precision.HIGHEST)  10.6 us
  transfers between devices with their start and end apart: 6, of which 5 were waited for; matrix products, arithmetic and copies ran while one was open for 6% of the time, Pallas kernels for 0%

commit v1 on v0

--- a/solution.py
+++ b/solution.py
@@ -18,7 +18,8 @@
 def gather_in_order(shard, axes, order):
     parts = shard[None]
     for k in order:
-        parts = lax.all_gather(parts, axes[k], axis=0, tiled=True)
+        sent = jnp.stack([parts] * lax.axis_size(axes[k]))
+        parts = jnp.concatenate(lax.all_to_all(sent, axes[k], 0, 0), axis=0)
     held = [lax.axis_size(axes[k]) for k in reversed(order)]
     parts = parts.reshape(*held, *shard.shape)
     turned = sorted(range(len(order)), key=lambda place: order[len(order) - 1 - place])

time: 481 us -> 434 us (0.902)
  waiting for transfers between devices: 186 us -> 123 us
  blocking collectives: 30.4 us -> 46.4 us
  between operations: 14.7 us -> 1.61 us
  starting transfers between devices: 5.42 us -> 16.5 us
  local copies, waits for them, and re-layouts: 44 us -> 49.2 us
    all_gather x4 -> x0, waiting for transfers between devices: 95.2 us -> none  [gather_in_order(): parts = lax.all_gather(parts, axes[k], axis=0, tiled=True)]
    all_to_all x0 -> x3, blocking collectives: none -> 46.4 us  [gather_in_order(): parts = jnp.concatenate(lax.all_to_all(sent, axes[k], 0, 0), axis=0)]
    all_to_all x0 -> x3, waiting for transfers between devices: none -> 37.3 us  [gather_in_order(): parts = jnp.concatenate(lax.all_to_all(sent, axes[k], 0, 0), axis=0)]
    all_gather x2 -> x0, blocking collectives: 30.4 us -> none  [gather_in_order(): parts = lax.all_gather(parts, axes[k], axis=0, tiled=True)]
    all_to_all x0 -> x3, starting transfers between devices: none -> 15.3 us  [gather_in_order(): parts = jnp.concatenate(lax.all_to_all(sent, axes[k], 0, 0), axis=0)]
    another operation x0 -> x8, local copies, waits for them, and re-layouts: none -> 11.5 us  [the longest x6 6.33 us: gather_in_order(): sent = jnp.stack([parts] * lax.axis_size(axes[k]))]
    reshape x2 -> x0, local copies, waits for them, and re-layouts: 10.5 us -> none  [gather_in_order(): parts = parts.reshape(*held, *shard.shape)]
    dot_general x2, matrix products: 16.5 us -> 10.6 us  [one_round(): jnp.einsum('nba,nbc->nac', pieces, row_slab, precision=lax.Precision.HIGH...]
  transfers between devices with their start and end apart: 6 -> 5, of which waited for: 5 -> 4; matrix products, arithmetic and copies ran while one was open for 6% -> 8% of each run, Pallas kernels for 0% -> 0%
where the time goes in v1:
time: 434 us; the launch traced here: 427 us
  other arithmetic  145 us (33%)
  waiting for transfers between devices  123 us (28%)
  local copies, waits for them, and re-layouts  49.2 us (11%)
  blocking collectives  46.4 us (11%)
  matrix products  45.5 us (10%)
  starting transfers between devices  16.5 us (4%)
    ppermute x2, waiting for transfers between devices, from_partner(): lax.ppermute(shard, axis, [(i, i ^ 1 << bit) for i in range(lax.axis_size...  86.1 us
    another operation x18, other arithmetic, cayley_sweeps(): lower_part = jnp.linalg.cholesky(system)  74.3 us
    another operation x12, other arithmetic, cayley_sweeps(): rotate_now = jax.scipy.linalg.cho_solve((lower_part, True), square_turn)  62.8 us
    all_to_all x3, blocking collectives, gather_in_order(): parts = jnp.concatenate(lax.all_to_all(sent, axes[k], 0, 0), axis=0)  46.4 us
    all_to_all x3, waiting for transfers between devices, gather_in_order(): parts = jnp.concatenate(lax.all_to_all(sent, axes[k], 0, 0), axis=0)  37.3 us
    all_to_all x3, starting transfers between devices, gather_in_order(): parts = jnp.concatenate(lax.all_to_all(sent, axes[k], 0, 0), axis=0)  15.3 us
    dot_general x2, matrix products, one_round(): columns = jnp.dot(current, rotate, precision=lax.Precision.HIGHEST)  13 us
    dot_general x2, matrix products, one_round(): basis = jnp.dot(basis, rotate, precision=lax.Precision.HIGHEST)  12.7 us
  transfers between devices with their start and end apart: 5, of which 4 were waited for; matrix products, arithmetic and copies ran while one was open for 8% of the time, Pallas kernels for 0%

profile of v1, /device:TPU:2, one launch (start us, length us, event | category | flops | bytes accessed | tf_op | source)
XLA Modules:
  0.0 427.5 jit_solution(3535773446599772634)
XLA Ops:
  3.7 11.7 %cholesky.104 = f32[128,128]{1,0:T(8,128)S(1)} custom-call(f32[128,128]{1,0:T(8,128)S(1)} %fusion.100), custom_call_target="Cholesky" | custom-call | tf_op jit(solution)/shard_map/jit(cholesky)/cholesky | solution.py:50
  16.8 9.8 %custom-call.24 = f32[1,128,128]{1,2,0:T(8,128)S(1)} custom-call(f32[1,128,128]{2,1,0:T(8,128)S(1)} %fusion.18), custom_call_target="InvertDiagBlocksLowerTriangular" | custom-call | tf_op jit(solution)/shard_map/jit(_cho_solve)/triangular_solve | solution.py:52
  30.3 11.7 %cholesky.115 = f32[128,128]{1,0:T(8,128)S(1)} custom-call(f32[128,128]{1,0:T(8,128)S(1)} %fusion.95), custom_call_target="Cholesky" | custom-call | tf_op jit(solution)/shard_map/jit(cholesky)/cholesky | solution.py:50
  43.3 9.8 %custom-call.25 = f32[1,128,128]{1,2,0:T(8,128)S(1)} custom-call(f32[1,128,128]{2,1,0:T(8,128)S(1)} %fusion.19), custom_call_target="InvertDiagBlocksLowerTriangular" | custom-call | tf_op jit(solution)/shard_map/jit(_cho_solve)/triangular_solve | solution.py:52
  57.0 11.7 %cholesky.126 = f32[128,128]{1,0:T(8,128)S(1)} custom-call(f32[128,128]{1,0:T(8,128)S(1)} %fusion.90), custom_call_target="Cholesky" | custom-call | tf_op jit(solution)/shard_map/jit(cholesky)/cholesky | solution.py:50
  70.0 9.8 %custom-call.26 = f32[1,128,128]{1,2,0:T(8,128)S(1)} custom-call(f32[1,128,128]{2,1,0:T(8,128)S(1)} %fusion.20), custom_call_target="InvertDiagBlocksLowerTriangular" | custom-call | tf_op jit(solution)/shard_map/jit(_cho_solve)/triangular_solve | solution.py:52
  80.7 14.6 %all_to_all.30 = f32[4,1,1,128,128]{3,4,2,1,0:T(8,128)S(1)} all-to-all(f32[4,1,1,128,128]{3,4,2,1,0:T(8,128)S(1)} %stack.18), channel_id=1, replica_groups=mesh['wide_0'=4,'wide_1'=4,'wide_2'=4,'layer'=4] {'wide_1'}, dimensions={0} | all-to-all | bytes 524288 | tf_op jit(solution)/shard_map/all_to_all | solution.py:22
  95.3 17.0 %all_to_all.31 = f32[4,4,1,128,128]{3,4,1,2,0:T(8,128)S(1)} all-to-all(f32[4,4,1,128,128]{3,4,1,2,0:T(8,128)S(1)} %stack.19), channel_id=1, replica_groups=mesh['wide_0'=4,'wide_1'=4,'wide_2'=4,'layer'=4] {'wide_0'}, dimensions={0} | all-to-all | bytes 2097152 | tf_op jit(solution)/shard_map/all_to_all | solution.py:22
  114.9 5.5 %all-to-all-start.2 = ((f32[4,16,1,128,128]{3,4,1,2,0:T(8,128)}), f32[4,16,1,128,128]{3,4,1,2,0:T(8,128)}, u32[]{:S(2)}, u32[]{:S(2)}) async-start(f32[4,16,1,128,128]{3,4,1,2,0:T(8,128)} %stack.20), calls=%async_computation.2 | async-start | bytes 8388608 | tf_op jit(solution)/shard_map/all_to_all | solution.py:22
  120.4 8.1 %convolution_bitcast_fusion = f32[8192,128]{0,1:T(8,128)} fusion(f32[128,128]{1,0:T(8,128)S(1)} %fusion.147, f32[8192,128]{1,0:T(8,128)} %param.4), kind=kOutput, calls=%fused_computation.6 | convolution fusion | flops 1610612736 | bytes 8454144 | tf_op jit(solution)/shard_map/dot_general | solution.py:73
  128.5 5.6 %copy.106 = f32[8192,128]{1,0:T(8,128)} copy(f32[8192,128]{0,1:T(8,128)} %convolution_bitcast_fusion) | data formatting | bytes 8388608 | tf_op jit(solution)/shard_map/reshape | solution.py:77
  134.1 30.6 %all-to-all-done.2 = f32[4,16,1,128,128]{3,4,1,2,0:T(8,128)} async-done(((f32[4,16,1,128,128]{3,4,1,2,0:T(8,128)}), f32[4,16,1,128,128]{3,4,1,2,0:T(8,128)}, u32[]{:S(2)}, u32[]{:S(2)}) %all-to-all-start.2) | async-done | bytes 4194336 | tf_op jit(solution)/shard_map/all_to_all | solution.py:22
  168.1 4.8 %fusion.148 = f32[64,128,128]{2,1,0:T(8,128)S(1)} fusion(f32[64,128,128]{1,2,0:T(8,128)S(1)} %bitcast.179, f32[64,128,128]{2,1,0:T(8,128)S(1)} %bitcast.177), kind=kOutput, calls=%fused_computation.227 | convolution fusion | flops 1610612736 | bytes 12582912 | tf_op jit(solution)/shard_map/nba,nbc->nac/dot_general | solution.py:78
  173.0 4.7 %fusion.141 = (f32[8192,64]{1,0:T(8,128)}, f32[8192,64]{1,0:T(8,128)}) fusion(f32[8192,128]{1,0:T(8,128)S(1)} %bitcast.174), kind=kLoop, calls=%fused_computation.220 | loop fusion | bytes 8388608 | tf_op jit(solution)/shard_map/slice | solution.py:100
  181.1 44.2 %collective-permute-done = f32[8192,64]{0,1:T(8,128)} collective-permute-done((f32[8192,64]{0,1:T(8,128)S(1)}, f32[8192,64]{0,1:T(8,128)}, u32[]{:S(2)}, u32[]{:S(2)}) %collective-permute-start) | collective-permute-done | bytes 2097184 | tf_op jit(solution)/shard_map/ppermute | solution.py:34
  225.3 4.0 copy.83
  229.3 4.6 %pad_maximum_fusion = f32[8192,128]{1,0:T(8,128)S(1)} fusion(f32[8192,64]{1,0:T(8,128)} %copy.83, f32[8192,64]{1,0:T(8,128)} %get-tuple-element.8), kind=kLoop, calls=%fused_computation.7 | loop fusion | flops 1048576 | bytes 8388608 | tf_op jit(solution)/shard_map/concatenate | solution.py:100
  243.7 11.7 %cholesky.137 = f32[128,128]{1,0:T(8,128)S(1)} custom-call(f32[128,128]{1,0:T(8,128)S(1)} %fusion.84), custom_call_target="Cholesky" | custom-call | tf_op jit(solution)/shard_map/jit(cholesky)/cholesky | solution.py:50
  256.8 9.8 %custom-call.27 = f32[1,128,128]{1,2,0:T(8,128)S(1)} custom-call(f32[1,128,128]{2,1,0:T(8,128)S(1)} %fusion.21), custom_call_target="InvertDiagBlocksLowerTriangular" | custom-call | tf_op jit(solution)/shard_map/jit(_cho_solve)/triangular_solve | solution.py:52
  270.4 11.7 %cholesky.148 = f32[128,128]{1,0:T(8,128)S(1)} custom-call(f32[128,128]{1,0:T(8,128)S(1)} %fusion.79), custom_call_target="Cholesky" | custom-call | tf_op jit(solution)/shard_map/jit(cholesky)/cholesky | solution.py:50
  283.4 9.8 %custom-call.28 = f32[1,128,128]{1,2,0:T(8,128)S(1)} custom-call(f32[1,128,128]{2,1,0:T(8,128)S(1)} %fusion.22), custom_call_target="InvertDiagBlocksLowerTriangular" | custom-call | tf_op jit(solution)/shard_map/jit(_cho_solve)/triangular_solve | solution.py:52
  296.7 11.7 %cholesky.159 = f32[128,128]{1,0:T(8,128)S(1)} custom-call(f32[128,128]{1,0:T(8,128)S(1)} %fusion.74), custom_call_target="Cholesky" | custom-call | tf_op jit(solution)/shard_map/jit(cholesky)/cholesky | solution.py:50
  309.8 9.8 %custom-call.29 = f32[1,128,128]{1,2,0:T(8,128)S(1)} custom-call(f32[1,128,128]{2,1,0:T(8,128)S(1)} %fusion.23), custom_call_target="InvertDiagBlocksLowerTriangular" | custom-call | tf_op jit(solution)/shard_map/jit(_cho_solve)/triangular_solve | solution.py:52
  320.4 14.7 %all_to_all.32 = f32[4,1,1,128,128]{3,4,2,1,0:T(8,128)S(1)} all-to-all(f32[4,1,1,128,128]{3,4,2,1,0:T(8,128)S(1)} %stack.21), channel_id=1, replica_groups=mesh['wide_0'=4,'wide_1'=4,'wide_2'=4,'layer'=4] {'wide_1'}, dimensions={0} | all-to-all | bytes 524288 | tf_op jit(solution)/shard_map/all_to_all | solution.py:22
  336.2 3.5 all-to-all-start.4
  339.8 4.2 fusion.4
  343.9 6.7 %all-to-all-done.4 = f32[4,4,1,128,128]{3,4,1,2,0:T(8,128)S(1)} async-done(((f32[4,4,1,128,128]{3,4,1,2,0:T(8,128)}), f32[4,4,1,128,128]{3,4,1,2,0:T(8,128)S(1)}, u32[]{:S(2)}, u32[]{:S(2)}) %all-to-all-start.4) | async-done | bytes 1048608 | tf_op jit(solution)/shard_map/all_to_all | solution.py:22
  353.2 6.3 %all-to-all-start.5 = ((f32[4,16,1,128,128]{3,4,1,2,0:T(8,128)}), f32[4,16,1,128,128]{3,4,1,2,0:T(8,128)}, u32[]{:S(2)}, u32[]{:S(2)}) async-start(f32[4,16,1,128,128]{3,4,1,2,0:T(8,128)} %stack.23), calls=%async_computation.5 | async-start | bytes 8388608 | tf_op jit(solution)/shard_map/all_to_all | solution.py:22
  362.7 41.9 %collective-permute-done.1 = f32[8192,64]{0,1:T(8,128)S(1)} collective-permute-done((f32[8192,64]{0,1:T(8,128)S(1)}, f32[8192,64]{0,1:T(8,128)S(1)}, u32[]{:S(2)}, u32[]{:S(2)}) %collective-permute-start.1) | collective-permute-done | bytes 2097184 | tf_op jit(solution)/shard_map/ppermute | solution.py:34
  404.6 8.6 %fusion = f32[8192,128]{1,0:T(8,128)} fusion(f32[128,128]{1,0:T(8,128)S(1)} %fusion.154, f32[8192,64]{0,1:T(8,128)S(1)} %collective-permute-done.1, f32[8192,64]{0,1:T(8,128)S(1)} %get-tuple-element.4), kind=kOutput, calls=%fused_computation.9 | convolution fusion | flops 1611661312 | bytes 8454144 | tf_op jit(solution)/shard_map/dot_general | solution.py:82
  413.1 4.9 %fusion.68 = f32[64,128,128]{2,1,0:T(8,128)} fusion(f32[64,128,128]{2,1,0:T(8,128)S(1)} %bitcast.176, f32[128,128]{1,0:T(8,128)S(1)} %fusion.154), kind=kOutput, calls=%fused_computation.127 | convolution fusion | flops 1610612736 | bytes 8454144 | tf_op jit(solution)/shard_map/dot_general | solution.py:73
  421.5 5.7 %fusion.155 = f32[64,128,128]{2,1,0:T(8,128)} fusion(f32[64,128,128]{1,2,0:T(8,128)S(1)} %bitcast.180, f32[64,128,128]{2,1,0:T(8,128)S(1)} %copy-done.2), kind=kOutput, calls=%fused_computation.234 | convolution fusion | flops 1610612736 | bytes 12582912 | tf_op jit(solution)/shard_map/nba,nbc->nac/dot_general | solution.py:78
  (118 shorter events, 56.5 us)
Async XLA Ops:
  114.9 49.8 %all-to-all-start.2 = ((f32[4,16,1,128,128]{3,4,1,2,0:T(8,128)}), f32[4,16,1,128,128]{3,4,1,2,0:T(8,128)}, u32[]{:S(2)}, u32[]{:S(2)}) async-start(f32[4,16,1,128,128]{3,4,1,2,0:T(8,128)} %stack.20), calls=%async_computation.2 | async-start | bytes 8388608 | tf_op jit(solution)/shard_map/all_to_all | solution.py:22
  164.7 3.4 copy-start.3
  180.5 44.8 %collective-permute-start = (f32[8192,64]{0,1:T(8,128)S(1)}, f32[8192,64]{0,1:T(8,128)}, u32[]{:S(2)}, u32[]{:S(2)}) collective-permute-start(f32[8192,64]{0,1:T(8,128)S(1)} %copy.82), channel_id=1, source_target_pairs={{0,128},{4,132},{8,136},{12,140},{16,144},{20,148},{24,152},{28,15... | collective-permute-start | bytes 6291464 | tf_op jit(solution)/shard_map/ppermute | solution.py:34
  239.5 2.0 copy-start
  336.2 14.4 %all-to-all-start.4 = ((f32[4,4,1,128,128]{3,4,1,2,0:T(8,128)}), f32[4,4,1,128,128]{3,4,1,2,0:T(8,128)S(1)}, u32[]{:S(2)}, u32[]{:S(2)}) async-start(f32[4,4,1,128,128]{3,4,1,2,0:T(8,128)} %stack.22), calls=%async_computation.4 | async-start | bytes 2097152 | tf_op jit(solution)/shard_map/all_to_all | solution.py:22
  353.2 64.8 %all-to-all-start.5 = ((f32[4,16,1,128,128]{3,4,1,2,0:T(8,128)}), f32[4,16,1,128,128]{3,4,1,2,0:T(8,128)}, u32[]{:S(2)}, u32[]{:S(2)}) async-start(f32[4,16,1,128,128]{3,4,1,2,0:T(8,128)} %stack.23), calls=%async_computation.5 | async-start | bytes 8388608 | tf_op jit(solution)/shard_map/all_to_all | solution.py:22
  362.0 42.5 %collective-permute-start.1 = (f32[8192,64]{0,1:T(8,128)S(1)}, f32[8192,64]{0,1:T(8,128)S(1)}, u32[]{:S(2)}, u32[]{:S(2)}) collective-permute-start(f32[8192,64]{0,1:T(8,128)S(1)} %get-tuple-element.5), channel_id=1, source_target_pairs={{0,128},{4,132},{8,136},{12,140},{16,144},{20,148},{24,152},{28,15... | collective-permute-start | bytes 6291464 | tf_op jit(solution)/shard_map/ppermute | solution.py:34
  404.6 8.6 %copy-start.1 = (f32[2,32,2,64,128]{4,3,2,1,0:T(8,128)S(1)}, f32[2,32,2,64,128]{4,3,2,1,0:T(8,128)}, u32[]{:S(2)}) copy-start(f32[2,32,2,64,128]{4,3,2,1,0:T(8,128)} %copy-done) | copy-start | bytes 12582916
  418.0 3.5 copy-start.2
